TPU v7x, 32 devices: a whole 2x2x4 slice. The times are simulated.
32 devices in a mesh: cols: 8 (over y, x, core), rows: 4 (over z).
Axes of the slice: x: 2, y: 2, z: 4, core: 2. Of those that a mesh axis runs over, the one named last changes fastest.
Arguments:
- weight: float32 [8192, 28672], P('rows', 'cols'), may hold values from -6 to 6
- scales: float32 [8192], P('rows'), may hold values from 0.2 to 0.5
- panels: float32 [1024, 28672], P('cols', 'rows')
- block_inverse: float32 [2, 128, 128], replicated
- grid_codes: int32 [16], replicated, may hold values from -12 to 12, as said below
- block_starts: int32 [2], replicated, may hold values from 0 to 25088, as said below
Outputs:
- result: float32 [8192, 28672], P('rows', 'cols')
Inputs may be any that keep to these rules, and one draw needn't show every extreme that they name: `grid_codes`: strictly increasing. `block_starts`: strictly increasing multiples of 3584; the last block starts at the last device's columns.
All inputs are finite; a program needn't handle non-finite values.
Results may differ from a plain program's by a relative error of at most 0.00012.
Values sent between devices are 32-bit elements; how exact they have to be, the bound alone decides.
A program may use at most 192 MiB of HBM per device.

v0:
```python
import functools

import jax
import jax.numpy as jnp
from jax import lax
from jax.experimental import pallas as pl
from jax.experimental.pallas import tpu as pltpu
from jax.sharding import PartitionSpec as P

BLK = 128
SUB = 32
LEVELS = 16
BLOCKS = 2
GROUPS = BLK // SUB

softness = 0.2
F32, BF16 = jnp.float32, jnp.bfloat16
MESH = pl.DeviceIdType.MESH


def split2(x):
    hi = x.astype(BF16)
    return hi, (x - hi.astype(F32)).astype(BF16)


def split3(x):
    hi = x.astype(BF16)
    rest = x - hi.astype(F32)
    mid = rest.astype(BF16)
    return hi, mid, (rest - mid.astype(F32)).astype(BF16)


def rounding_rows(inverse, diag_block):
    rows = lax.broadcasted_iota(jnp.int32, (BLK, BLK), 0) // SUB
    cols = lax.broadcasted_iota(jnp.int32, (BLK, BLK), 1) // SUB
    inv = jnp.where(rows == cols, inverse, 0.0)
    later = jnp.where(cols > rows, diag_block, 0.0)
    return inv + jnp.dot(
        inv, later, precision=lax.Precision.HIGHEST, preferred_element_type=F32
    )


def inner_block(block_t, scale, codes_ref, g_ref, base):
    levels = [codes_ref[k].astype(F32) for k in range(LEVELS)]
    sharp = 0.5 / softness
    center = 0.5 * (levels[0] + levels[LEVELS - 1])
    half = [0.5 * (levels[k + 1] - levels[k]) for k in range(LEVELS - 1)]
    mids = [sharp * 0.5 * (levels[k] + levels[k + 1]) for k in range(LEVELS - 1)]
    gain = sharp / scale
    groups = [block_t[j * SUB : (j + 1) * SUB, :] for j in range(GROUPS)]
    errors = []
    for j in range(GROUPS):
        current = groups[j]
        ratio = current * gain
        total = jnp.zeros_like(current) + center
        for k in range(LEVELS - 1):
            total = total + half[k] * jnp.tanh(ratio - mids[k])
        quantized = total * scale
        h, m, l = split3(current - quantized)
        stacked = jnp.concatenate([h, m, h, l, h, m, l, m], axis=0)
        moved = jnp.dot(g_ref[base + j], stacked, preferred_element_type=F32)
        errors.append(moved[j * SUB : (j + 1) * SUB, :])
        for i in range(j + 1, GROUPS):
            groups[i] = groups[i] - moved[i * SUB : (i + 1) * SUB, :]
        groups[j] = quantized
    return jnp.concatenate(groups, axis=0), jnp.concatenate(errors, axis=0)


def round_kernel(
    chunk, meta_ref, codes_ref, inv_ref, diag_ref, p0_ref, p1_ref, scale_ref, wblk_ref, w_ref, out_ref,
    pcat, gcat, ecat, block
):
    step = pl.program_id(0)
    cols_per = w_ref.shape[1]
    first = meta_ref[0]
    cut0, cut1 = meta_ref[1] + BLK, meta_ref[2] + BLK
    is_first = first == meta_ref[1]
    is_last = first == meta_ref[2]

    @pl.when(step == 0)
    def _():
        @pl.loop(0, cols_per // chunk)
        def _(i):
            at = pl.ds(pl.multiple_of(i * chunk, chunk), chunk)
            ids = first + i * chunk + lax.broadcasted_iota(jnp.int32, (BLK, chunk), 1)
            for b, (p_ref, cut) in enumerate(((p0_ref, cut0), (p1_ref, cut1))):
                hi, lo = split2(jnp.where(ids >= cut, p_ref[:, at], 0.0))
                pcat[b * BLK : (b + 1) * BLK, at] = hi
                pcat[(2 + b) * BLK : (3 + b) * BLK, at] = lo
                pcat[(4 + b) * BLK : (5 + b) * BLK, at] = hi

        for b in range(BLOCKS):
            diag = diag_ref[...] if b == 0 else p1_ref[:, :BLK]
            pieces = split3(rounding_rows(inv_ref[b], diag))
            h, m, l = [piece.astype(F32) for piece in pieces]
            for j in range(GROUPS):
                at = slice(j * SUB, (j + 1) * SUB)
                stacked = jnp.concatenate(
                    [h[at], h[at], m[at], h[at], l[at], m[at], m[at], l[at]], axis=0
                )
                gcat[b * GROUPS + j] = stacked.T.astype(BF16)
        ecat[...] = jnp.zeros_like(ecat)

    def put_errors(b, errors_t):
        hi, lo = split2(errors_t.T)
        ecat[:, b * BLK : (b + 1) * BLK] = hi
        ecat[:, (2 + b) * BLK : (3 + b) * BLK] = hi
        ecat[:, (4 + b) * BLK : (5 + b) * BLK] = lo

    scale = scale_ref[...]
    rounded, errors = inner_block(wblk_ref[...].T, scale, codes_ref, gcat, 0)
    put_errors(0, errors)
    block[...] = rounded

    @pl.when(is_last)
    def _():
        change = jnp.zeros((w_ref.shape[0], BLK), F32)
        for k in (0, 2, 4):
            at = slice(k * BLK, (k + 1) * BLK)
            change += jnp.dot(ecat[:, at], pcat[at, :BLK], preferred_element_type=F32)
        current = w_ref[:, :BLK] - change
        rounded, errors = inner_block(current.T, scale, codes_ref, gcat, GROUPS)
        put_errors(1, errors)
        block[...] = rounded

    @pl.loop(0, cols_per // chunk)
    def _(i):
        at = pl.ds(pl.multiple_of(i * chunk, chunk), chunk)
        out_ref[:, at] = w_ref[:, at] - jnp.dot(
            ecat[...], pcat[:, at], preferred_element_type=F32
        )

    @pl.when(jnp.logical_or(is_first, is_last))
    def _():
        out_ref[:, :BLK] = block[...].T


def round_local(meta, grid_codes, block_inverse, diag, p0, p1, scales, wblk, weight):
    rows, cols_per = weight.shape
    tile = next(t for t in (512, 256, 128, 64, 32, 16, 8) if rows % t == 0)
    chunk = next(c for c in (512, 256, 128) if cols_per % c == 0)
    smem = pl.BlockSpec(memory_space=pltpu.SMEM)

    def whole(shape):
        return pl.BlockSpec(shape, lambda i: (0,) * len(shape))

    return pl.pallas_call(
        functools.partial(round_kernel, chunk),
        grid=(rows // tile,),
        out_shape=jax.ShapeDtypeStruct(weight.shape, F32),
        in_specs=[
            smem,
            smem,
            whole((BLOCKS, BLK, BLK)),
            whole((BLK, BLK)),
            whole((BLK, cols_per)),
            whole((BLK, cols_per)),
            pl.BlockSpec((1, tile), lambda i: (0, i)),
            pl.BlockSpec((tile, BLK), lambda i: (i, 0)),
            pl.BlockSpec((tile, cols_per), lambda i: (i, 0)),
        ],
        out_specs=pl.BlockSpec((tile, cols_per), lambda i: (i, 0)),
        scratch_shapes=[
            pltpu.VMEM((6 * BLK, cols_per), BF16),
            pltpu.VMEM((BLOCKS * GROUPS, BLK, 8 * SUB), BF16),
            pltpu.VMEM((tile, 6 * BLK), BF16),
            pltpu.VMEM((BLK, tile), F32),
        ],
        compiler_params=pltpu.CompilerParams(
            dimension_semantics=("arbitrary",), vmem_limit_bytes=60 * 1024 * 1024
        ),
        name="round_local",
    )(meta, grid_codes, block_inverse, diag, p0, p1, scales[None, :], wblk, weight)


def spread_kernel(
    pieces, ratio, last_only, with_diag, x_ref, d_ref, out_ref, dout_ref,
    held, slots, recv_sem, up_sem, down_sem, dsend_sem, drecv_sem
):
    rows, cols = lax.axis_size("rows"), lax.axis_size("cols")
    me, col = lax.axis_index("rows"), lax.axis_index("cols")
    holder = col // ratio
    depth = x_ref.shape[0] // pieces

    barrier = pltpu.get_barrier_semaphore()
    for step in range(1, rows):
        other = lax.rem(me + step, rows)
        pl.semaphore_signal(barrier, inc=1, device_id=(col, other), device_id_type=MESH)
    pl.semaphore_wait(barrier, rows - 1)

    def part(ref, i):
        return ref.at[pl.ds(i * depth, depth)]

    def copy(source, i, sems, target):
        return pltpu.make_async_remote_copy(
            src_ref=part(source, i),
            dst_ref=part(held, i),
            send_sem=sems.at[i],
            recv_sem=recv_sem.at[i],
            device_id=(col, target),
            device_id_type=MESH,
        )

    def diag_copy(step):
        other = lax.rem(me + step, rows)
        return pltpu.make_async_remote_copy(
            src_ref=d_ref,
            dst_ref=slots.at[step - 1],
            send_sem=dsend_sem.at[step - 1],
            recv_sem=drecv_sem.at[step - 1],
            device_id=(col, other),
            device_id_type=MESH,
        )

    if with_diag:
        for step in range(1, rows):
            diag_copy(step).start()

    active = col == cols - 1 if last_only else col >= 0
    goes_up = jnp.logical_and(me >= holder, me < rows - 1)
    goes_down = jnp.logical_and(me <= holder, me > 0)
    up = lax.rem(me + 1, rows)
    down = lax.rem(me + rows - 1, rows)

    @pl.when(active)
    def _():
        @pl.when(me == holder)
        def _():
            for i in range(pieces):
                @pl.when(goes_up)
                def _():
                    copy(x_ref, i, up_sem, up).start()

                @pl.when(goes_down)
                def _():
                    copy(x_ref, i, down_sem, down).start()

            out_ref[...] = x_ref[...]

        @pl.when(me != holder)
        def _():
            for i in range(pieces):
                copy(held, i, up_sem, up).wait_recv()

                @pl.when(goes_up)
                def _():
                    copy(held, i, up_sem, up).start()

                @pl.when(goes_down)
                def _():
                    copy(held, i, down_sem, down).start()

                at = slice(i * depth, (i + 1) * depth)
                out_ref[at, :] = held[at, :]

        for i in range(pieces):
            @pl.when(goes_up)
            def _():
                copy(held, i, up_sem, up).wait_send()

            @pl.when(goes_down)
            def _():
                copy(held, i, down_sem, down).wait_send()

    if last_only:
        @pl.when(jnp.logical_not(active))
        def _():
            out_ref[...] = x_ref[...]

    if with_diag:
        total = d_ref[...]
        for step in range(1, rows):
            diag_copy(step).wait()
            total = total + slots[step - 1]
        dout_ref[...] = total
    else:
        dout_ref[...] = d_ref[...]


def spread(x, diag, ratio, last_only, with_diag, collective_id):
    rows = lax.axis_size("rows")
    pieces = 16
    vmem = pl.BlockSpec(memory_space=pltpu.VMEM)
    sems = pltpu.SemaphoreType.DMA
    return pl.pallas_call(
        functools.partial(spread_kernel, pieces, ratio, last_only, with_diag),
        out_shape=(
            jax.ShapeDtypeStruct(x.shape, F32),
            jax.ShapeDtypeStruct(diag.shape, F32),
        ),
        in_specs=[vmem, vmem],
        out_specs=(vmem, vmem),
        scratch_shapes=[
            pltpu.VMEM(x.shape, F32),
            pltpu.VMEM((rows - 1,) + diag.shape, F32),
            sems((pieces,)),
            sems((pieces,)),
            sems((pieces,)),
            sems((rows - 1,)),
            sems((rows - 1,)),
        ],
        compiler_params=pltpu.CompilerParams(
            collective_id=collective_id, has_side_effects=True
        ),
        cost_estimate=pl.CostEstimate(
            flops=0, bytes_accessed=64 * x.size * 4, transcendentals=0
        ),
        name="spread",
    )(x, diag)


def local(weight, scales, panels, block_inverse, grid_codes, block_starts):
    cols_per = weight.shape[1]
    slab_width = panels.shape[1]
    own, row = lax.axis_index("cols"), lax.axis_index("rows")
    first = own * cols_per
    ratio = slab_width // cols_per
    offset = first % slab_width
    start0, start1 = block_starts[0], block_starts[1]
    mine = own == start0 // cols_per
    slab, wblk = lax.psum(
        (jnp.where(mine, panels, 0.0), jnp.where(mine, weight[:, :BLK], 0.0)), "cols"
    )
    none = jnp.zeros((8, BLK), F32)
    own1 = lax.dynamic_slice_in_dim(panels, offset, cols_per, 1)
    p1, _ = spread(own1, none, ratio, True, False, 1)
    own0 = lax.dynamic_slice_in_dim(slab, offset, cols_per, 1)
    diag = lax.dynamic_slice_in_dim(slab, start0 % slab_width, BLK, 1)
    diag = jnp.where(row == start0 // slab_width, diag, 0.0)
    p0, diag = spread(own0, diag, ratio, False, True, 2)
    meta = jnp.stack([first, start0, start1]).astype(jnp.int32)
    return round_local(meta, grid_codes, block_inverse, diag, p0, p1, scales, wblk, weight)


def solution(mesh):
    placed = (P("rows", "cols"), P("rows"), P("cols", "rows"), P(), P(), P())
    return jax.shard_map(
        local, mesh=mesh, in_specs=placed, out_specs=P("rows", "cols"), check_vma=False
    )
```

profile of v0, /device:TPU:7, one launch (start us, length us, event | category | flops | bytes accessed | tf_op | source)
XLA Modules:
  0.0 206.8 jit_solution(9004958407224225533)
XLA Ops:
  6.5 0.0 all-reduce.3.cloned.1.call-start
  8.5 2.3 %slice_select_fusion = f32[2048,128]{1,0:T(8,128)} fusion(f32[2048,3584]{1,0:T(8,128)} %w_ref.1, pred[]{:T(512)S(6)} %eq.9), kind=kLoop, calls=%fused_computation.1 | loop fusion | flops 262144 | bytes 2097153 | tf_op jit(solution)/shard_map/jit(_where)/select_n | solution.py:322
  10.8 2.2 %broadcast_select_fusion = f32[128,7168]{1,0:T(8,128)} fusion(f32[128,7168]{1,0:T(8,128)} %param.8, pred[]{:T(512)S(6)} %eq.9), kind=kLoop, calls=%fused_computation | loop fusion | flops 917504 | bytes 7340033 | tf_op jit(solution)/shard_map/jit(_where)/select_n | solution.py:322
  13.0 0.0 copy-start
  13.0 0.0 all-reduce.3.cloned.1.call-update
  13.1 0.6 copy-done
  13.8 3.3 %constant_dynamic-slice_fusion.x_ref = f32[128,3584]{1,0:T(8,128)} fusion(f32[128,7168]{1,0:T(8,128)} %param.8, s32[]{:T(128)S(6)} %select_n.53), kind=kLoop, calls=%fused_computation.3 | loop fusion | bytes 3670020 | tf_op jit(solution)/shard_map/dynamic_slice | solution.py:325
  17.1 0.6 broadcast_in_dim.20.d_ref
  17.7 33.1 %spread.3 = (f32[128,3584]{1,0:T(8,128)}, f32[8,128]{1,0:T(8,128)}) custom-call(f32[128,3584]{1,0:T(8,128)} %constant_dynamic-slice_fusion.x_ref, f32[8,128]{1,0:T(8,128)} %broadcast_in_dim.20.d_ref), custom_call_target="tpu_custom_call" | custom-call | bytes 117440512 | tf_op jit(solution)/shard_map/spread/pallas_call | solution.py:285
  50.8 0.6 pad_add_fusion.meta_ref
  51.4 49.3 %all-reduce.3.cloned.1.call-done = (f32[128,7168]{1,0:T(8,128)}, f32[2048,128]{1,0:T(8,128)}) async-done(((f32[128,7168]{1,0:T(8,128)}, f32[2048,128]{1,0:T(8,128)}), (f32[128,7168]{1,0:T(8,128)}, f32[2048,128]{1,0:T(8,128)})) %all-reduce.3.cloned.1.call-update) | async-done | bytes 4718608 | tf_op jit(solution)/shard_map/psum | solution.py:321
  100.7 3.3 %constant_dynamic-slice_fusion.1.x_ref = f32[128,3584]{1,0:T(8,128)} fusion(f32[128,7168]{1,0:T(8,128)} %get-tuple-element.11, s32[]{:T(128)S(6)} %select_n.53), kind=kLoop, calls=%fused_computation.4 | loop fusion | bytes 3670020 | tf_op jit(solution)/shard_map/dynamic_slice | solution.py:327
  104.0 1.6 dynamic-slice_select_fusion.d_ref
  105.6 56.3 %spread.2 = (f32[128,3584]{1,0:T(8,128)}, f32[128,128]{1,0:T(8,128)}) custom-call(f32[128,3584]{1,0:T(8,128)} %constant_dynamic-slice_fusion.1.x_ref, f32[128,128]{1,0:T(8,128)} %dynamic-slice_select_fusion.d_ref), custom_call_target="tpu_custom_call" | custom-call | bytes 117440512 | tf_op jit(solution)/shard_map/spread/pallas_call | solution.py:285
  161.9 38.0 %round_local.1 = f32[2048,3584]{1,0:T(8,128)} custom-call(s32[3]{0:T(128)} %pad_add_fusion.meta_ref, s32[16]{0:T(128)} %codes_ref.1, f32[2,128,128]{2,1,0:T(8,128)} %inv_ref.1, f32[128,128]{1,0:T(8,128)} %get-tuple-element.8.diag_ref, f32[128,3584]{1,0:T(8,128)} %get-tuple-element.9.p0_ref, f32[128,3584]{1,0:T(8,128)} %get-tuple-element.10.p1_ref, ...), custom_call_target="tpu_custom_call" | custom-call | tf_op jit(solution)/shard_map/round_local/pallas_call | solution.py:147
Async XLA Ops:
  6.5 94.2 %all-reduce.3.cloned.1.call-start = ((), (), s32[]{:S(2)}) async-start(), calls=%async_computation | async-start | bytes 9437184 | tf_op jit(solution)/shard_map/psum | solution.py:321
  13.0 0.7 copy-start
Sparse Core Ops, SparseCore 0:
  13.2 87.4 all-reduce.2
where the time goes:
time: 207 us
  Pallas kernels  127 us (61%)
  waiting for transfers between devices  49.3 us (24%)
  between operations  15.5 us (7%)
  local copies, waits for them, and re-layouts  7.78 us (4%)
  other arithmetic  6.74 us (3%)
    pallas_call x2, Pallas kernels, spread(): pl.pallas_call(functools.partial(spread_kernel, pieces, ratio, last_only,...  89.4 us
    psum x1, waiting for transfers between devices, local(): lax.psum((jnp.where(mine, panels, 0.0), jnp.where(mine, weight[:, :BLK],...  49.3 us
    pallas_call x1, Pallas kernels, round_local(): pl.pallas_call(functools.partial(round_kernel, chunk), grid=(rows // tile...  38 us
  transfers between devices with their start and end apart: 1, of which 1 were waited for; matrix products, arithmetic and copies ran while one was open for 2% of the time, Pallas kernels for 16%

commit v1 on v0

v1 whole, which is shorter than its diff:
```python
import functools

import jax
import jax.numpy as jnp
from jax import lax
from jax.experimental import pallas as pl
from jax.experimental.pallas import tpu as pltpu
from jax.sharding import PartitionSpec as P

BLK = 128
SUB = 32
LEVELS = 16
GROUPS = BLK // SUB
CH = 8
ETILE = 512

softness = 0.2
F32, BF16 = jnp.float32, jnp.bfloat16
MESH = pl.DeviceIdType.MESH


def split2(x):
    hi = x.astype(BF16)
    return hi, (x - hi.astype(F32)).astype(BF16)


def split3(x):
    hi = x.astype(BF16)
    rest = x - hi.astype(F32)
    mid = rest.astype(BF16)
    return hi, mid, (rest - mid.astype(F32)).astype(BF16)


def rounding_rows(inverse, diag_block):
    rows = lax.broadcasted_iota(jnp.int32, (BLK, BLK), 0) // SUB
    cols = lax.broadcasted_iota(jnp.int32, (BLK, BLK), 1) // SUB
    inv = jnp.where(rows == cols, inverse, 0.0)
    later = jnp.where(cols > rows, diag_block, 0.0)
    return inv + jnp.dot(
        inv, later, precision=lax.Precision.HIGHEST, preferred_element_type=F32
    )


def inner_block(block_t, scale, codes_ref, g_ref, b):
    levels = [codes_ref[k].astype(F32) for k in range(LEVELS)]
    sharp = 0.5 / softness
    center = 0.5 * (levels[0] + levels[LEVELS - 1])
    half = [0.5 * (levels[k + 1] - levels[k]) for k in range(LEVELS - 1)]
    mids = [sharp * 0.5 * (levels[k] + levels[k + 1]) for k in range(LEVELS - 1)]
    gain = sharp / scale
    groups = [block_t[j * SUB : (j + 1) * SUB, :] for j in range(GROUPS)]
    errors = []
    for j in range(GROUPS):
        current = groups[j]
        ratio = current * gain
        total = jnp.zeros_like(current) + center
        for k in range(LEVELS - 1):
            total = total + half[k] * jnp.tanh(ratio - mids[k])
        quantized = total * scale
        h, m, l = split3(current - quantized)
        stacked = jnp.concatenate([h, m, h, l, h, m, l, m], axis=0)
        moved = jnp.dot(g_ref[b, j], stacked, preferred_element_type=F32)
        errors.append(moved[j * SUB : (j + 1) * SUB, :])
        for i in range(j + 1, GROUPS):
            groups[i] = groups[i] - moved[i * SUB : (i + 1) * SUB, :]
        groups[j] = quantized
    return jnp.concatenate(groups, axis=0), jnp.concatenate(errors, axis=0)


def put_rounding(g_ref, b, inverse, diag):
    h, m, l = [piece.astype(F32) for piece in split3(rounding_rows(inverse, diag))]
    for j in range(GROUPS):
        at = slice(j * SUB, (j + 1) * SUB)
        stacked = jnp.concatenate(
            [h[at], h[at], m[at], h[at], l[at], m[at], m[at], l[at]], axis=0
        )
        g_ref[b, j] = stacked.T.astype(BF16)


def lookup(table, index):
    value = jnp.int32(table[0])
    for i in range(1, len(table)):
        value = jnp.where(index == i, jnp.int32(table[i]), value)
    return value


def move_kernel(
    o, N, R, codes_ref, inv_ref, scale_ref, pan_ref, w_ref,
    land, e0, e1, block, wv,
    gcat, diag, cross, xcat, wblk, rblk,
    rrecv, drecv, qrecv, up_s, dn_s, del_s, scat_s, qscat_s,
    era, erb, esa, esb, pa, pb, dsem, dsend, xsem, xsend, wrecv, wsend, bsem, lsem
):
    col, me = lax.axis_index("cols"), lax.axis_index("rows")
    cols_per = w_ref.shape[1]
    ratio = pan_ref.shape[1] // cols_per
    last = N - 1
    chips = N // 2
    m = BLK // chips // CH
    n_chunks = BLK // CH
    nt = w_ref.shape[0] // ETILE
    hpart = ETILE // 2
    oh, oq, lq = o // ratio, o // 2, chips - 1
    k0 = o % 2
    k1 = 1 - k0
    first_at, second_at = 2 * oq + k1, 2 * lq + k1
    q, k = col // 2, col % 2
    partner = q * 2 + 1 - k
    carrier = k == k0
    is_owner, is_last = col == o, col == last
    rounds_first, rounds_second = col == first_at, col == second_at

    barrier = pltpu.get_barrier_semaphore()
    for step in range(1, N):
        pl.semaphore_signal(
            barrier, inc=1, device_id=(lax.rem(col + step, N), me), device_id_type=MESH
        )
    for step in range(1, R):
        pl.semaphore_signal(
            barrier, inc=1, device_id=(col, lax.rem(me + step, R)), device_id_type=MESH
        )
    pl.semaphore_wait(barrier, N - 1 + R - 1)

    def both(*terms):
        value = terms[0]
        for term in terms[1:]:
            value = jnp.logical_and(value, term)
        return value

    def remote(src, dst, ssem, rsem, to):
        return pltpu.make_async_remote_copy(
            src_ref=src, dst_ref=dst, send_sem=ssem, recv_sem=rsem,
            device_id=to, device_id_type=MESH,
        )

    def rows_at(slot):
        return land.at[pl.ds(pl.multiple_of(slot * CH, CH), CH)]

    def slot0(chip, s, i):
        return jnp.where(chip * 2 + k0 == s, chip * m + i, 2 * n_chunks + s * m + i)

    def slot1(chip, i):
        own = chip * 2 + k0 == last
        return jnp.where(own, n_chunks + chip * m + i, 2 * n_chunks + N * m + i)

    def pan(j, kk):
        return pan_ref.at[pl.ds(pl.multiple_of(j * CH, CH), CH), pl.ds(kk * cols_per, cols_per)]

    def corner(kk):
        return pan_ref.at[:, pl.ds(kk * cols_per, BLK)]

    def first_cols():
        return w_ref.at[:, pl.ds(0, BLK)]

    to_first, to_second = (first_at, me), (second_at, me)
    w_first = remote(first_cols(), wblk.at[0], wsend.at[0], wrecv.at[0], to_first)
    d_first = remote(corner(o % ratio), diag.at[0], dsend.at[0], dsem.at[0], to_first)
    x_second = remote(corner(last % ratio), cross, xsend.at[0], xsem, to_second)
    if second_at == last:
        w_second = pltpu.make_async_copy(first_cols(), wblk.at[1], wrecv.at[1])
        d_second = pltpu.make_async_copy(corner(last % ratio), diag.at[1], dsem.at[1])
    else:
        w_second = remote(first_cols(), wblk.at[1], wsend.at[1], wrecv.at[1], to_second)
        d_second = remote(corner(last % ratio), diag.at[1], dsend.at[R], dsem.at[1], to_second)

    def pass_on(ref, ssem, rsem, step):
        return remote(ref, ref, ssem, rsem, (col, lax.rem(me + step, R)))

    def pass_diag(b, step):
        return pass_on(diag.at[b], dsend.at[b * R + step], dsem.at[b], step)

    def pass_cross(step):
        return pass_on(cross, xsend.at[step], xsem, step)

    def arrived(ref, sem):
        return remote(ref, ref, dsend.at[0], sem, (partner, me))

    top = me == R - 1

    @pl.when(both(is_owner, me == oh))
    def _():
        d_first.start()

    @pl.when(is_owner)
    def _():
        w_first.start()

    @pl.when(both(is_owner, top))
    def _():
        x_second.start()

    @pl.when(both(is_last, top))
    def _():
        d_second.start()

    @pl.when(is_last)
    def _():
        w_second.start()

    flows = ratio * m

    def scatter(chip, n):
        kk, i = lax.rem(n, ratio), n // ratio
        s = me * ratio + kk
        return (chip * m + i, kk, rows_at(slot0(chip, s, i)), s * m + i)

    def scatter_to(chip, n):
        j, kk, dst, f = scatter(chip, n)
        return remote(
            pan_at(j, kk), dst, scat_s.at[n * chips + chip], rrecv.at[f], (chip * 2 + k0, me)
        )

    def scatter_own(n):
        j, kk, dst, f = scatter(oq, n)
        return pltpu.make_async_copy(pan_at(j, kk), dst, rrecv.at[f])

    def pan_at(j, kk):
        return pan_ref.at[
            pl.ds(pl.multiple_of(j * CH, CH), CH),
            pl.ds(pl.multiple_of(kk * cols_per, BLK), cols_per),
        ]

    def scatter1(chip, i):
        return remote(
            pan(chip * m + i, last % ratio), rows_at(slot1(chip, i)),
            qscat_s.at[i * chips + chip], rrecv.at[N * m + i], (chip * 2 + k0, me),
        )

    def scatter1_own(i):
        return pltpu.make_async_copy(
            pan(lq * m + i, last % ratio), rows_at(slot1(lq, i)), rrecv.at[N * m + i]
        )

    p1_local = pltpu.make_async_copy(
        pan_ref.at[:, pl.ds((last % ratio) * cols_per, cols_per)],
        land.at[pl.ds(BLK, BLK)], lsem.at[1],
    )

    def own_row(j):
        return pltpu.make_async_copy(pan(j, o % ratio), rows_at(j), drecv.at[j])

    @pl.when(is_owner)
    def _():
        @pl.loop(0, flows)
        def _(n):
            @pl.when(me * ratio + lax.rem(n, ratio) >= o)
            def _():
                scatter_own(n).start()

                @pl.loop(1, chips)
                def _(step):
                    scatter_to(lax.rem(oq + step, chips), n).start()

        @pl.when(me == oh)
        def _():
            for j in range(n_chunks):
                if j // m != oq:
                    own_row(j).start()

    @pl.when(both(is_last, top))
    def _():
        p1_local.start()

        @pl.loop(0, m)
        def _(i):
            if k0 == 0:
                scatter1(lq, i).start()

            @pl.loop(1, chips)
            def _(step):
                scatter1(lax.rem(lq + step, chips), i).start()

    wcopy = pltpu.make_async_copy(w_ref, wv, lsem.at[0])
    wcopy.start()

    order = [c ^ (c >> 1) for c in range(chips)]
    where = [order.index(c) for c in range(chips)]
    pos = lookup(where, q)
    spot = lax.rem(pos - where[oq] + chips, chips)
    fwd_chip = lookup(order, lax.rem(pos + 1, chips))
    bwd_chip = lookup(order, lax.rem(pos + chips - 1, chips))
    ends = (chips - 1, 1)

    def epart(t, half):
        return e0.at[pl.ds(pl.multiple_of(t * ETILE + half * hpart, hpart), hpart)]

    def ring(t, half):
        to = fwd_chip if half == 0 else bwd_chip
        ss, rs = (esa, era) if half == 0 else (esb, erb)
        return remote(epart(t, half), epart(t, half), ss.at[t], rs.at[t], (to * 2 + k, me))

    def across(t, half):
        ss, rs = (pa, era) if half == 0 else (pb, erb)
        return remote(epart(t, half), epart(t, half), ss.at[t], rs.at[t], (partner, me))

    def send_errors(t):
        for half in range(2):
            ring(t, half).start()
            across(t, half).start()

    b_first = remote(rblk.at[0], block, bsem.at[0], bsem.at[1], (o, me))
    e_second = remote(e1, e1, bsem.at[2], bsem.at[3], (last, me))
    b_second = remote(rblk.at[1], block, bsem.at[4], bsem.at[5], (last, me))

    @pl.when(rounds_first)
    def _():
        arrived(diag.at[0], dsem.at[0]).wait_recv()

        @pl.when(me == oh)
        def _():
            for step in range(1, R):
                pass_diag(0, step).start()

        w_first.wait_recv()

    @pl.when(rounds_second)
    def _():
        arrived(diag.at[1], dsem.at[1]).wait_recv()
        arrived(cross, xsem).wait_recv()

        @pl.when(top)
        def _():
            for step in range(1, R):
                pass_diag(1, step).start()
                pass_cross(step).start()

        arrived(wblk.at[1], wrecv.at[1]).wait_recv()
        xh, xl = split2(cross[...])
        xcat[...] = jnp.concatenate([xh, xh, xl], axis=0)

    @pl.loop(0, 2)
    def _(b):
        @pl.when(jnp.logical_or(both(b == 0, rounds_first), both(b == 1, rounds_second)))
        def _():
            put_rounding(gcat, b, inv_ref[b], diag[b])

    lag = jnp.where(rounds_first, 0, jnp.maximum(spot, chips - spot))

    def relay_errors(t, half):
        @pl.when(both(t >= 0, t < nt))
        def _():
            ring(t, half).wait_recv()

            @pl.when(spot != ends[half])
            def _():
                ring(t, half).start()

            across(t, half).start()

    @pl.when(jnp.logical_not(carrier))
    def _():
        @pl.loop(0, 2 * (nt + chips))
        def _(turn):
            now, b = turn // 2, lax.rem(turn, 2)
            t = jnp.where(b == 0, now, now - lag)
            inside = both(t >= 0, t < nt)
            at = pl.ds(pl.multiple_of(t * ETILE, ETILE), ETILE)

            @pl.when(both(b == 1, jnp.logical_not(rounds_first)))
            def _():
                relay_errors(now - spot, 0)
                relay_errors(now - chips + spot, 1)

            @pl.when(both(b == 1, rounds_second, inside))
            def _():
                eh, el = split2(e0[at, :])
                wblk[1, at, :] = wblk[1, at, :] - jnp.dot(
                    jnp.concatenate([eh, el, eh], axis=1), xcat[...], preferred_element_type=F32
                )

            mine = jnp.logical_or(both(b == 0, rounds_first), both(b == 1, rounds_second))

            @pl.when(both(mine, inside))
            def _():
                rounded, errors = inner_block(
                    wblk[b, at, :].T, scale_ref[:, at], codes_ref, gcat, b
                )
                rblk[b, at, :] = rounded.T
                errors = errors.T

                @pl.when(b == 0)
                def _():
                    e0[at, :] = errors

                @pl.when(b == 1)
                def _():
                    e1[at, :] = errors

            @pl.when(both(b == 1, rounds_first, now > 0, now <= nt))
            def _():
                send_errors(now - 1)

    @pl.when(rounds_first)
    def _():
        b_first.start()

    @pl.when(rounds_second)
    def _():
        if second_at != last:
            e_second.start()
            b_second.start()
        else:
            block[...] = rblk[1]

    def relay(n, d, sign):
        kk, i = lax.rem(n, ratio), n // ratio
        h = me + sign * d
        s = h * ratio + kk
        f = s * m + i
        valid = both(n >= 0, n < flows, s >= o)
        if sign < 0:
            valid = both(valid, h >= 0)
        if sign > 0:
            valid = both(valid, h < R)
        buf = rows_at(slot0(q, s, i))

        def hop(sem, step):
            return remote(buf, buf, sem.at[f], rrecv.at[f], (col, me + step))

        deliver = remote(
            buf, rows_at(q * m + i), del_s.at[f], drecv.at[q * m + i], (s, me)
        )
        goes = col != s
        if sign == 0:
            goes = both(goes, jnp.logical_or(s != o, me != oh))
        return valid, goes, hop(up_s, 1), hop(dn_s, -1), deliver

    def relay_start(n, d, sign):
        valid, goes, up, down, deliver = relay(n, d, sign)

        @pl.when(valid)
        def _():
            up.wait_recv()
            if sign <= 0:
                @pl.when(me < R - 1)
                def _():
                    up.start()
            if sign >= 0:
                @pl.when(me > 0)
                def _():
                    down.start()

            @pl.when(goes)
            def _():
                deliver.start()

    def relay_end(n, d, sign):
        valid, goes, up, down, deliver = relay(n, d, sign)

        @pl.when(valid)
        def _():
            if sign <= 0:
                @pl.when(me < R - 1)
                def _():
                    up.wait_send()
            if sign >= 0:
                @pl.when(me > 0)
                def _():
                    down.wait_send()

            @pl.when(goes)
            def _():
                deliver.wait_send()

    def relay1(i):
        f = N * m + i
        buf = rows_at(slot1(q, i))
        down = remote(buf, buf, dn_s.at[f], rrecv.at[f], (col, me - 1))
        deliver = remote(
            buf, rows_at(n_chunks + q * m + i), del_s.at[f], qrecv.at[q * m + i], (last, me)
        )
        return down, deliver, both(me < R - 1, col != last)

    at_source = both(is_last, top)

    def relay1_start(i):
        down, deliver, goes = relay1(i)

        @pl.when(jnp.logical_not(at_source))
        def _():
            down.wait_recv()

        @pl.when(both(at_source, i == 0))
        def _():
            p1_local.wait()

        @pl.when(me > 0)
        def _():
            down.start()

        @pl.when(goes)
        def _():
            deliver.start()

    def relay1_end(i):
        down, deliver, goes = relay1(i)

        @pl.when(me > 0)
        def _():
            down.wait_send()

        @pl.when(goes)
        def _():
            deliver.wait_send()

    def walk(one, other):
        @pl.loop(0, flows + 2 * R)
        def _(level):
            for d in range(R):
                for sign in (0,) if d == 0 else (-1, 1):
                    one(level - d, d, sign)
            turn = level - (R - 1 - me)

            @pl.when(both(turn >= 0, lax.rem(turn + 2 * R, 2) == 0, turn < 2 * m))
            def _():
                other(turn // 2)

    @pl.when(carrier)
    def _():
        walk(relay_start, relay1_start)
        walk(relay_end, relay1_end)

    @pl.when(jnp.logical_not(carrier))
    def _():
        @pl.loop(0, nt)
        def _(t):
            for half in range(2):
                @pl.when(jnp.logical_or(rounds_first, spot != ends[half]))
                def _():
                    ring(t, half).wait_send()

                across(t, half).wait_send()

    @pl.when(carrier)
    def _():
        @pl.loop(0, nt)
        def _(t):
            for half in range(2):
                across(t, half).wait_recv()

    @pl.when(is_owner)
    def _():
        w_first.wait_send()
        b_first.wait_recv()

        @pl.loop(0, flows)
        def _(n):
            @pl.when(me * ratio + lax.rem(n, ratio) >= o)
            def _():
                @pl.loop(1, chips)
                def _(step):
                    scatter_to(lax.rem(oq + step, chips), n).wait_send()

    @pl.when(both(is_owner, me == oh))
    def _():
        d_first.wait_send()

    @pl.when(both(is_owner, top))
    def _():
        x_second.wait_send()

    @pl.when(rounds_first)
    def _():
        b_first.wait_send()

        @pl.when(me == oh)
        def _():
            for step in range(1, R):
                pass_diag(0, step).wait_send()

    @pl.when(both(rounds_second, top))
    def _():
        for step in range(1, R):
            pass_diag(1, step).wait_send()
            pass_cross(step).wait_send()

    if second_at != last:
        @pl.when(rounds_second)
        def _():
            e_second.wait_send()
            b_second.wait_send()

        @pl.when(is_last)
        def _():
            w_second.wait_send()
            e_second.wait_recv()
            b_second.wait_recv()

        @pl.when(both(is_last, top))
        def _():
            d_second.wait_send()

    @pl.when(both(is_last, top))
    def _():
        if k0 == 0:
            p1_local.wait()

        @pl.loop(0, m)
        def _(i):
            if k0 == 0:
                scatter1(lq, i).wait_send()

            @pl.loop(1, chips)
            def _(step):
                scatter1(lax.rem(lq + step, chips), i).wait_send()

    @pl.loop(0, n_chunks)
    def _(j):
        carried = (j // m) * 2 + k0

        @pl.when(both(col >= o, col != carried))
        def _():
            arrived(rows_at(j), drecv.at[j]).wait_recv()

        @pl.when(both(is_last, me < R - 1, carried != last))
        def _():
            arrived(rows_at(n_chunks + j), qrecv.at[j]).wait_recv()

    wcopy.wait()


def move(o, N, R, codes, inverse, scales, panels, weight):
    rows, cols_per = weight.shape
    chips = N // 2
    m = BLK // chips // CH
    ratio = panels.shape[1] // cols_per
    n_chunks = BLK // CH
    n_rel = (N + 1) * m
    nt = rows // ETILE
    hbm = pl.BlockSpec(memory_space=pltpu.HBM)
    vmem = pl.BlockSpec(memory_space=pltpu.VMEM)
    smem = pl.BlockSpec(memory_space=pltpu.SMEM)
    dma = pltpu.SemaphoreType.DMA
    return pl.pallas_call(
        functools.partial(move_kernel, o, N, R),
        out_shape=(
            pltpu.VMEM((2 * BLK + n_rel * CH, cols_per), F32),
            pltpu.VMEM((rows, BLK), F32),
            pltpu.VMEM((rows, BLK), F32),
            pltpu.VMEM((rows, BLK), F32),
            pltpu.VMEM((rows, cols_per), F32),
        ),
        in_specs=[smem, vmem, vmem, hbm, hbm],
        out_specs=(vmem,) * 5,
        scratch_shapes=[
            pltpu.VMEM((2, GROUPS, BLK, 8 * SUB), BF16),
            pltpu.VMEM((2, BLK, BLK), F32),
            pltpu.VMEM((BLK, BLK), F32),
            pltpu.VMEM((3 * BLK, BLK), BF16),
            pltpu.VMEM((2, rows, BLK), F32),
            pltpu.VMEM((2, rows, BLK), F32),
            dma((n_rel,)), dma((n_chunks,)), dma((n_chunks,)),
            dma((n_rel,)), dma((n_rel,)), dma((n_rel,)),
            dma((ratio * m * chips,)), dma((m * chips,)),
            dma((nt,)), dma((nt,)), dma((nt,)), dma((nt,)), dma((nt,)), dma((nt,)),
            dma((2,)), dma((2 * R,)), dma, dma((R,)), dma((2,)), dma((2,)), dma((6,)), dma((2,)),
        ],
        compiler_params=pltpu.CompilerParams(
            collective_id=o + 1, has_side_effects=True, vmem_limit_bytes=20 * 1024 * 1024
        ),
        name=f"move_{o}",
    )(codes, inverse, scales[None, :], panels, weight)


def apply_kernel(o, N, col_ref, land, e0, e1, block, wv, out_ref, pcat, ecat, obuf, sems):
    rows, cols_per = wv.shape
    tile = obuf.shape[1]
    chunk = obuf.shape[2]
    slots = obuf.shape[0]
    col = col_ref[0]
    is_owner = col == o
    is_last = col == N - 1
    touched = col >= o
    nr, nc = rows // tile, cols_per // chunk

    def put_panel(b):
        @pl.loop(0, nc)
        def _(i):
            at = pl.ds(pl.multiple_of(i * chunk, chunk), chunk)
            hi, lo = split2(land[b * BLK : (b + 1) * BLK, at])
            pcat[3 * b * BLK : (3 * b + 1) * BLK, at] = hi
            pcat[(3 * b + 1) * BLK : (3 * b + 2) * BLK, at] = hi
            pcat[(3 * b + 2) * BLK : (3 * b + 3) * BLK, at] = lo

    def clear_panel(b):
        pcat[3 * b * BLK : (3 * b + 3) * BLK, :BLK] = jnp.zeros((3 * BLK, BLK), BF16)

    def put_errors(b, ref):
        hi, lo = split2(ref[...])
        ecat[:, 3 * b * BLK : (3 * b + 1) * BLK] = hi
        ecat[:, (3 * b + 1) * BLK : (3 * b + 2) * BLK] = lo
        ecat[:, (3 * b + 2) * BLK : (3 * b + 3) * BLK] = hi

    @pl.when(touched)
    def _():
        put_panel(0)
        put_errors(0, e0)

    @pl.when(is_owner)
    def _():
        clear_panel(0)

    @pl.when(is_last)
    def _():
        put_panel(1)
        clear_panel(1)
        put_errors(1, e1)

    def out_copy(step):
        slot = lax.rem(step, slots)
        c, r = step // nr, lax.rem(step, nr)
        return pltpu.make_async_copy(
            obuf.at[slot],
            out_ref.at[
                pl.ds(pl.multiple_of(r * tile, tile), tile),
                pl.ds(pl.multiple_of(c * chunk, chunk), chunk),
            ],
            sems.at[slot],
        )

    @pl.loop(0, nr * nc)
    def _(step):
        slot = lax.rem(step, slots)
        c, r = step // nr, lax.rem(step, nr)
        at_r = pl.ds(pl.multiple_of(r * tile, tile), tile)
        at_c = pl.ds(pl.multiple_of(c * chunk, chunk), chunk)

        @pl.when(step >= slots)
        def _():
            out_copy(step - slots).wait()

        @pl.when(is_last)
        def _():
            obuf[slot] = wv[at_r, at_c] - jnp.dot(
                ecat[at_r, :], pcat[:, at_c], preferred_element_type=F32
            )

        @pl.when(jnp.logical_and(touched, jnp.logical_not(is_last)))
        def _():
            obuf[slot] = wv[at_r, at_c] - jnp.dot(
                ecat[at_r, : 3 * BLK], pcat[: 3 * BLK, at_c], preferred_element_type=F32
            )

        @pl.when(jnp.logical_not(touched))
        def _():
            obuf[slot] = wv[at_r, at_c]

        @pl.when(jnp.logical_and(c == 0, jnp.logical_or(is_owner, is_last)))
        def _():
            obuf[slot, :, :BLK] = block[at_r, :]

        out_copy(step).start()

    for k in range(slots):
        out_copy(nr * nc - slots + k).wait()


def apply(o, N, col, land, e0, e1, block, wv):
    rows, cols_per = wv.shape
    tile = next(t for t in (512, 256, 128, 64, 32, 16, 8) if rows % t == 0)
    chunk = next(c for c in (512, 256, 128) if cols_per % c == 0)
    slots = 4
    vmem = pl.BlockSpec(memory_space=pltpu.VMEM)
    return pl.pallas_call(
        functools.partial(apply_kernel, o, N),
        out_shape=pltpu.HBM((rows, cols_per), F32),
        in_specs=[pl.BlockSpec(memory_space=pltpu.SMEM)] + [vmem] * 5,
        out_specs=pl.BlockSpec(memory_space=pltpu.HBM),
        scratch_shapes=[
            pltpu.VMEM((6 * BLK, cols_per), BF16),
            pltpu.VMEM((rows, 6 * BLK), BF16),
            pltpu.VMEM((slots, tile, chunk), F32),
            pltpu.SemaphoreType.DMA((slots,)),
        ],
        compiler_params=pltpu.CompilerParams(vmem_limit_bytes=22 * 1024 * 1024),
        name=f"apply_{o}",
    )(col, land, e0, e1, block, wv)


def local(N, R, weight, scales, panels, block_inverse, grid_codes, block_starts):
    cols_per = weight.shape[1]
    owner = block_starts[0] // cols_per

    def branch(o):
        def run(weight, scales, panels, inverse, codes):
            parts = move(o, N, R, codes, inverse, scales, panels, weight)
            col = lax.axis_index("cols").astype(jnp.int32)[None]
            parts = [pltpu.with_memory_space_constraint(x, pltpu.VMEM) for x in parts]
            return apply(o, N, col, *parts)
        return run

    return lax.switch(
        owner, [branch(o) for o in range(N - 1)],
        weight, scales, panels, block_inverse, grid_codes,
    )


def solution(mesh):
    N, R = mesh.shape["cols"], mesh.shape["rows"]
    placed = (P("rows", "cols"), P("rows"), P("cols", "rows"), P(), P(), P())
    return jax.shard_map(
        functools.partial(local, N, R), mesh=mesh, in_specs=placed,
        out_specs=P("rows", "cols"), check_vma=False,
    )
```

time: 207 us -> 85.8 us (0.41)
  Pallas kernels: 127 us -> 75.8 us
  waiting for transfers between devices: 49.3 us -> 0 us
  between operations: 15.5 us -> 2.17 us
  other arithmetic: 6.74 us -> 0 us
    pallas_call x3 -> x2, Pallas kernels: 127 us -> 75.8 us  [the longest x1 56.7 us: move(): pl.pallas_call(functools.partial(move_kernel, o, N, R), out_shape=(pltpu....]
    psum x1 -> x0, waiting for transfers between devices: 49.3 us -> none  [local(): lax.psum((jnp.where(mine, panels, 0.0), jnp.where(mine, weight[:, :BLK],...]
    dynamic_slice x2 -> x0, local copies, waits for them, and re-layouts: 6.58 us -> none  [the longest x1 3.31 us: local(): own1 = lax.dynamic_slice_in_dim(panels, offset, cols_per, 1)]
    cond x0 -> x4, local copies, waits for them, and re-layouts: none -> 6.41 us
    select_n x3 -> x0, other arithmetic: 6.15 us -> none  [the longest x1 2.33 us: local(): jnp.where(mine, weight[:, :BLK], 0.0)]
  transfers between devices with their start and end apart: 1 -> 0, of which waited for: 1 -> 0; matrix products, arithmetic and copies ran while one was open for 2% -> 0% of each run, Pallas kernels for 16% -> 0%
where the time goes in v1:
time: 85.8 us; the launch traced here: 84.9 us
  Pallas kernels  75.8 us (88%)
  local copies, waits for them, and re-layouts  6.41 us (7%)
  between operations  2.17 us (3%)
    pallas_call x1, Pallas kernels, move(): pl.pallas_call(functools.partial(move_kernel, o, N, R), out_shape=(pltpu....  56.7 us
    pallas_call x1, Pallas kernels, apply(): pl.pallas_call(functools.partial(apply_kernel, o, N), out_shape=pltpu.HBM...  19.1 us
    cond x4, local copies, waits for them, and re-layouts  6.41 us

profile of v1, /device:TPU:7, one launch (start us, length us, event | category | flops | bytes accessed | tf_op | source)
XLA Modules:
  0.0 84.9 jit_solution(3697140275073523197)
XLA Ops:
  2.0 82.7 %conditional.1 = (f32[2048,3584]{1,0:T(8,128)}) conditional(s32[]{:T(128)} %clamp.3, (f32[2048]{0:T(1024)}, s32[16]{0:T(128)}, f32[2,128,128]{2,1,0:T(8,128)}, f32[128,7168]{1,0:T(8,128)}, f32[2048,3584]{1,0:T(8,128)}) %tuple.26, (f32[2048]{0:T(1024)}, s32[16]{0:T(128)}, f32[2,128,128]{2,1,0:T(8,128)}, ...), branch_computations={%region_0.1_spmd, %region_1.2_spmd, %region_2.3_spmd, %region_3.4_... | conditional | flops 3 | bytes 62390368 | solution.py:792
  2.0 56.7 %move_2.1 = (f32[544,3584]{1,0:T(8,128)S(1)}, f32[2048,128]{1,0:T(8,128)S(1)}, f32[2048,128]{1,0:T(8,128)S(1)}, f32[2048,128]{1,0:T(8,128)S(1)}, f32[2048,3584]{1,0:T(8,128)S(1)}) custom-call(s32[16]{0:T(128)} %get-tuple-element.103.codes_ref, f32[2,128,128]{2,1,0:T(8,128)} %get-tuple-element.104.inv_ref, f32[1,2048]{1,0:T(1,128)} %bitcast.19, ...), custom_call_target="tpu_custom_call" | custom-call | tf_op jit(solution)/shard_map/cond/branch_2_fun/move_2/pallas_call | solution.py:634
  58.7 0.0 copy-start.4
  58.7 3.2 %copy-done.4 = f32[544,3584]{1,0:T(8,128)} copy-done((f32[544,3584]{1,0:T(8,128)}, f32[544,3584]{1,0:T(8,128)S(1)}, u32[]{:S(2)}) %copy-start.4) | copy-done | bytes 7798808 | tf_op jit(solution)/shard_map/cond
  61.9 0.0 copy-start.5
  61.9 3.2 %copy-done.5 = f32[544,3584]{1,0:T(8,128)S(1)} copy-done((f32[544,3584]{1,0:T(8,128)S(1)}, f32[544,3584]{1,0:T(8,128)}, u32[]{:S(2)}) %copy-start.5) | copy-done | bytes 7798808 | tf_op jit(solution)/shard_map/cond
  65.1 19.1 %apply_2.1 = f32[2048,3584]{1,0:T(8,128)} custom-call(s32[1]{0:T(128)} %bitcast.4.col_ref, f32[544,3584]{1,0:T(8,128)S(1)} %copy-done.5, f32[2048,128]{1,0:T(8,128)S(1)} %get-tuple-element.109.e0, f32[2048,128]{1,0:T(8,128)S(1)} %get-tuple-element.110.e1, f32[2048,128]{1,0:T(8,128)S(1)} %get-tuple-element.111.block, f32[2048,3584]{1,0:T(8,128)S(1)} %get-tuple-element.112.wv), custom_call_target="tpu_custom_call" | custom-call | tf_op jit(solution)/shard_map/cond/branch_2_fun/apply_2/pallas_call | solution.py:764
Async XLA Ops:
  58.7 3.2 %copy-start.4 = (f32[544,3584]{1,0:T(8,128)}, f32[544,3584]{1,0:T(8,128)S(1)}, u32[]{:S(2)}) copy-start(f32[544,3584]{1,0:T(8,128)S(1)} %get-tuple-element.108.land) | copy-start | bytes 23396356 | tf_op jit(solution)/shard_map/cond
  61.9 3.2 %copy-start.5 = (f32[544,3584]{1,0:T(8,128)S(1)}, f32[544,3584]{1,0:T(8,128)}, u32[]{:S(2)}) copy-start(f32[544,3584]{1,0:T(8,128)} %copy-done.4) | copy-start | bytes 23396356 | tf_op jit(solution)/shard_map/cond

commit v2 on v1

--- a/solution.py
+++ b/solution.py
@@ -89,7 +89,7 @@
     land, e0, e1, block, wv,
     gcat, diag, cross, xcat, wblk, rblk,
     rrecv, drecv, qrecv, up_s, dn_s, del_s, scat_s, qscat_s,
-    era, erb, esa, esb, pa, pb, dsem, dsend, xsem, xsend, wrecv, wsend, bsem, lsem
+    era, erb, esa, esb, pa, pb, es2, er2, bs2, br2, dsem, dsend, xsem, xsend, wrecv, wsend, bsem, lsem
 ):
     col, me = lax.axis_index("cols"), lax.axis_index("rows")
     cols_per = w_ref.shape[1]
@@ -101,6 +101,8 @@
     nt = w_ref.shape[0] // ETILE
     hpart = ETILE // 2
     oh, oq, lq = o // ratio, o // 2, chips - 1
+    m1 = n_chunks // 2
+    nq = lq ^ (chips // 2 if oq == lq else 1)
     k0 = o % 2
     k1 = 1 - k0
     first_at, second_at = 2 * oq + k1, 2 * lq + k1
@@ -139,9 +141,10 @@
     def slot0(chip, s, i):
         return jnp.where(chip * 2 + k0 == s, chip * m + i, 2 * n_chunks + s * m + i)
 
-    def slot1(chip, i):
-        own = chip * 2 + k0 == last
-        return jnp.where(own, n_chunks + chip * m + i, 2 * n_chunks + N * m + i)
+    def slot1(side, i):
+        if k0 == 1:
+            return jnp.where(side == 0, n_chunks + i, 2 * n_chunks + N * m + i)
+        return 2 * n_chunks + N * m + i
 
     def pan(j, kk):
         return pan_ref.at[pl.ds(pl.multiple_of(j * CH, CH), CH), pl.ds(kk * cols_per, cols_per)]
@@ -220,15 +223,10 @@
             pl.ds(pl.multiple_of(kk * cols_per, BLK), cols_per),
         ]
 
-    def scatter1(chip, i):
+    def scatter1(side, i):
         return remote(
-            pan(chip * m + i, last % ratio), rows_at(slot1(chip, i)),
-            qscat_s.at[i * chips + chip], rrecv.at[N * m + i], (chip * 2 + k0, me),
-        )
-
-    def scatter1_own(i):
-        return pltpu.make_async_copy(
-            pan(lq * m + i, last % ratio), rows_at(slot1(lq, i)), rrecv.at[N * m + i]
+            pan(side * m1 + i, last % ratio), rows_at(slot1(side, i)),
+            qscat_s.at[i * 2 + side], rrecv.at[N * m + i], ((lq, nq)[side] * 2 + k0, me),
         )
 
     p1_local = pltpu.make_async_copy(
@@ -261,14 +259,11 @@
     def _():
         p1_local.start()
 
-        @pl.loop(0, m)
+        @pl.loop(0, m1)
         def _(i):
             if k0 == 0:
-                scatter1(lq, i).start()
-
-            @pl.loop(1, chips)
-            def _(step):
-                scatter1(lax.rem(lq + step, chips), i).start()
+                scatter1(0, i).start()
+            scatter1(1, i).start()
 
     wcopy = pltpu.make_async_copy(w_ref, wv, lsem.at[0])
     wcopy.start()
@@ -299,8 +294,16 @@
             across(t, half).start()
 
     b_first = remote(rblk.at[0], block, bsem.at[0], bsem.at[1], (o, me))
-    e_second = remote(e1, e1, bsem.at[2], bsem.at[3], (last, me))
-    b_second = remote(rblk.at[1], block, bsem.at[4], bsem.at[5], (last, me))
+    def tile_of(ref, t):
+        return ref.at[pl.ds(pl.multiple_of(t * ETILE, ETILE), ETILE)]
+
+    def e_second(t):
+        return remote(tile_of(e1, t), tile_of(e1, t), es2.at[t], er2.at[t], (last, me))
+
+    def b_second(t):
+        return remote(
+            tile_of(rblk.at[1], t), tile_of(block, t), bs2.at[t], br2.at[t], (last, me)
+        )
 
     @pl.when(rounds_first)
     def _():
@@ -349,7 +352,7 @@
 
     @pl.when(jnp.logical_not(carrier))
     def _():
-        @pl.loop(0, 2 * (nt + chips))
+        @pl.loop(0, 2 * (nt + chips) + 1)
         def _(turn):
             now, b = turn // 2, lax.rem(turn, 2)
             t = jnp.where(b == 0, now, now - lag)
@@ -386,6 +389,12 @@
                 def _():
                     e1[at, :] = errors
 
+            if second_at != last:
+                @pl.when(both(b == 0, rounds_second, now > lag, now <= lag + nt))
+                def _():
+                    e_second(now - lag - 1).start()
+                    b_second(now - lag - 1).start()
+
             @pl.when(both(b == 1, rounds_first, now > 0, now <= nt))
             def _():
                 send_errors(now - 1)
@@ -396,10 +405,7 @@
 
     @pl.when(rounds_second)
     def _():
-        if second_at != last:
-            e_second.start()
-            b_second.start()
-        else:
+        if second_at == last:
             block[...] = rblk[1]
 
     def relay(n, d, sign):
@@ -464,10 +470,12 @@
 
     def relay1(i):
         f = N * m + i
-        buf = rows_at(slot1(q, i))
+        side = jnp.where(q == lq, 0, 1)
+        buf = rows_at(slot1(side, i))
         down = remote(buf, buf, dn_s.at[f], rrecv.at[f], (col, me - 1))
+        j = side * m1 + i
         deliver = remote(
-            buf, rows_at(n_chunks + q * m + i), del_s.at[f], qrecv.at[q * m + i], (last, me)
+            buf, rows_at(n_chunks + j), del_s.at[f], qrecv.at[j], (last, me)
         )
         return down, deliver, both(me < R - 1, col != last)
 
@@ -511,9 +519,9 @@
                     one(level - d, d, sign)
             turn = level - (R - 1 - me)
 
-            @pl.when(both(turn >= 0, lax.rem(turn + 2 * R, 2) == 0, turn < 2 * m))
-            def _():
-                other(turn // 2)
+            @pl.when(both(turn >= 0, turn < m1, jnp.logical_or(q == lq, q == nq)))
+            def _():
+                other(turn)
 
     @pl.when(carrier)
     def _():
@@ -577,14 +585,19 @@
     if second_at != last:
         @pl.when(rounds_second)
         def _():
-            e_second.wait_send()
-            b_second.wait_send()
+            @pl.loop(0, nt)
+            def _(t):
+                e_second(t).wait_send()
+                b_second(t).wait_send()
 
         @pl.when(is_last)
         def _():
             w_second.wait_send()
-            e_second.wait_recv()
-            b_second.wait_recv()
+
+            @pl.loop(0, nt)
+            def _(t):
+                e_second(t).wait_recv()
+                b_second(t).wait_recv()
 
         @pl.when(both(is_last, top))
         def _():
@@ -595,14 +608,11 @@
         if k0 == 0:
             p1_local.wait()
 
-        @pl.loop(0, m)
+        @pl.loop(0, m1)
         def _(i):
             if k0 == 0:
-                scatter1(lq, i).wait_send()
-
-            @pl.loop(1, chips)
-            def _(step):
-                scatter1(lax.rem(lq + step, chips), i).wait_send()
+                scatter1(0, i).wait_send()
+            scatter1(1, i).wait_send()
 
     @pl.loop(0, n_chunks)
     def _(j):
@@ -612,7 +622,9 @@
         def _():
             arrived(rows_at(j), drecv.at[j]).wait_recv()
 
-        @pl.when(both(is_last, me < R - 1, carried != last))
+        from_other = j >= m1 if k0 == 1 else j >= 0
+
+        @pl.when(both(is_last, me < R - 1, from_other))
         def _():
             arrived(rows_at(n_chunks + j), qrecv.at[j]).wait_recv()
 
@@ -625,7 +637,7 @@
     m = BLK // chips // CH
     ratio = panels.shape[1] // cols_per
     n_chunks = BLK // CH
-    n_rel = (N + 1) * m
+    n_rel = N * m + n_chunks // 2
     nt = rows // ETILE
     hbm = pl.BlockSpec(memory_space=pltpu.HBM)
     vmem = pl.BlockSpec(memory_space=pltpu.VMEM)
@@ -651,12 +663,13 @@
             pltpu.VMEM((2, rows, BLK), F32),
             dma((n_rel,)), dma((n_chunks,)), dma((n_chunks,)),
             dma((n_rel,)), dma((n_rel,)), dma((n_rel,)),
-            dma((ratio * m * chips,)), dma((m * chips,)),
+            dma((ratio * m * chips,)), dma((n_chunks,)),
             dma((nt,)), dma((nt,)), dma((nt,)), dma((nt,)), dma((nt,)), dma((nt,)),
-            dma((2,)), dma((2 * R,)), dma, dma((R,)), dma((2,)), dma((2,)), dma((6,)), dma((2,)),
+            dma((nt,)), dma((nt,)), dma((nt,)), dma((nt,)),
+            dma((2,)), dma((2 * R,)), dma, dma((R,)), dma((2,)), dma((2,)), dma((2,)), dma((2,)),
         ],
         compiler_params=pltpu.CompilerParams(
-            collective_id=o + 1, has_side_effects=True, vmem_limit_bytes=20 * 1024 * 1024
+            collective_id=o + 1, has_side_effects=True, vmem_limit_bytes=18 * 1024 * 1024
         ),
         name=f"move_{o}",
     )(codes, inverse, scales[None, :], panels, weight)
@@ -772,7 +785,7 @@
             pltpu.VMEM((slots, tile, chunk), F32),
             pltpu.SemaphoreType.DMA((slots,)),
         ],
-        compiler_params=pltpu.CompilerParams(vmem_limit_bytes=22 * 1024 * 1024),
+        compiler_params=pltpu.CompilerParams(vmem_limit_bytes=18 * 1024 * 1024),
         name=f"apply_{o}",
     )(col, land, e0, e1, block, wv)
 

time: 85.8 us -> 78.3 us (0.913)
  the two profiles are of different devices: /device:TPU:7 before, /device:TPU:23 now
where the time goes in v2:
time: 78.3 us; the launch traced here: 77.3 us
  Pallas kernels  74.6 us (95%)
  between operations  2.17 us (3%)
    pallas_call x1, Pallas kernels, move(): pl.pallas_call(functools.partial(move_kernel, o, N, R), out_shape=(pltpu....  55.5 us
    pallas_call x1, Pallas kernels, apply(): pl.pallas_call(functools.partial(apply_kernel, o, N), out_shape=pltpu.HBM...  19.1 us

profile of v2, /device:TPU:23, one launch (start us, length us, event | category | flops | bytes accessed | tf_op | source)
XLA Modules:
  0.0 77.3 jit_solution(12362384749942929113)
XLA Ops:
  2.0 75.1 %conditional.1 = (f32[2048,3584]{1,0:T(8,128)}) conditional(s32[]{:T(128)} %clamp.3, (f32[2048]{0:T(1024)}, s32[16]{0:T(128)}, f32[2,128,128]{2,1,0:T(8,128)}, f32[128,7168]{1,0:T(8,128)}, f32[2048,3584]{1,0:T(8,128)}) %tuple.26, (f32[2048]{0:T(1024)}, s32[16]{0:T(128)}, f32[2,128,128]{2,1,0:T(8,128)}, ...), branch_computations={%region_0.1_spmd, %region_1.2_spmd, %region_2.3_spmd, %region_3.4_... | conditional | flops 3 | bytes 40 | solution.py:805
  2.2 55.5 %move_3.1 = (f32[576,3584]{1,0:T(8,128)S(1)}, f32[2048,128]{1,0:T(8,128)S(1)}, f32[2048,128]{1,0:T(8,128)S(1)}, f32[2048,128]{1,0:T(8,128)S(1)}, f32[2048,3584]{1,0:T(8,128)S(1)}) custom-call(s32[16]{0:T(128)} %get-tuple-element.113.codes_ref, f32[2,128,128]{2,1,0:T(8,128)} %get-tuple-element.114.inv_ref, f32[1,2048]{1,0:T(1,128)} %bitcast.20, ...), custom_call_target="tpu_custom_call" | custom-call | tf_op jit(solution)/shard_map/cond/branch_3_fun/move_3/pallas_call | solution.py:646
  57.7 19.1 %apply_3.1 = f32[2048,3584]{1,0:T(8,128)} custom-call(s32[1]{0:T(128)} %bitcast.6.col_ref, f32[576,3584]{1,0:T(8,128)S(1)} %get-tuple-element.118.land, f32[2048,128]{1,0:T(8,128)S(1)} %get-tuple-element.119.e0, f32[2048,128]{1,0:T(8,128)S(1)} %get-tuple-element.120.e1, f32[2048,128]{1,0:T(8,128)S(1)} %get-tuple-element.121.block, ...), custom_call_target="tpu_custom_call" | custom-call | tf_op jit(solution)/shard_map/cond/branch_3_fun/apply_3/pallas_call | solution.py:777
